TPU v7x, 32 devices: a whole 2x2x4 slice. The times are simulated.
32 devices in a mesh: dp: 8 (over y, x, core), fsdp: 4 (over z).
Axes of the slice: x: 2, y: 2, z: 4, core: 2. Of those that a mesh axis runs over, the one named last changes fastest.
Arguments:
- tokens: bfloat16 [4096, 4096], P('dp'), may hold values from -6 to 6
- counts: int32 [8], P('dp'), may hold values from 256 to 512, as said below
- patch_index: int32 [4096], P('dp'), may hold values from 0 to 255
- clip_limit: float32 [], replicated, may hold values from 1024 to 8192
- norm_gain: float32 [4, 4096], replicated, may hold values from 0.25 to 1.75
- params: float32 [4, 4096, 4096], P(None, 'dp', 'fsdp'), may hold values from -0.09375 to 0.09375
- moments: float32 [4, 4096, 4096], P(None, 'dp', 'fsdp'), may hold values from -0.3 to 0.3
- seconds: float32 [4, 4096, 4096], P(None, 'dp', 'fsdp'), may hold values from 0.05 to 1
- gradients: float32 [4, 4096, 4096], P(None, 'dp', 'fsdp'), may hold values from -48 to 48
Outputs:
- params_new: float32 [4, 4096, 4096], P(None, 'dp', 'fsdp')
- moments_new: float32 [4, 4096, 4096], P(None, 'dp', 'fsdp')
- seconds_new: float32 [4, 4096, 4096], P(None, 'dp', 'fsdp')
- mixed: bfloat16 [4096, 4096], P('dp', 'fsdp')
Inputs may be any that keep to these rules, and one draw needn't show every extreme that they name: `counts`: at most 512, reached on some index of dp in every draw.
All inputs are finite; a program needn't handle non-finite values.
Results may differ from a plain program's by a relative error of at most 0.0095.
Values may be sent and summed in bfloat16 or wider, within the bound.
A program may use at most 192 MiB of HBM per device.

v0:
```python
import jax
import jax.numpy as jnp
from jax import lax
from jax.sharding import PartitionSpec as P

D = 4096
LAYERS = 4
GRID = 16
STEP = 40
beta_one = 0.9
beta_two = 0.95
adam_eps = 1e-08
learning_rate = 0.0024
weight_decay = 0.05
norm_eps = 1e-06


def position_code(patch_index):
    quarter = D // 4
    freqs = 1.0 / 10000.0 ** (jnp.arange(quarter, dtype=jnp.float32) / quarter)
    across = (patch_index // GRID).astype(jnp.float32)[:, None] * freqs[None, :]
    downward = (patch_index % GRID).astype(jnp.float32)[:, None] * freqs[None, :]
    return jnp.concatenate(
        [jnp.sin(across), jnp.cos(across), jnp.sin(downward), jnp.cos(downward)], axis=1
    )


def layer_norm(stream, gain_row):
    centre = jnp.mean(stream, axis=1, keepdims=True)
    shifted = stream - centre
    spread = jnp.mean(shifted * shifted, axis=1, keepdims=True)
    return (shifted * lax.rsqrt(spread + norm_eps) * gain_row[None, :]).astype(jnp.bfloat16)


def adam_update(params, moments, seconds, gradients, factor):
    clipped = gradients * factor
    moments_new = beta_one * moments + (1.0 - beta_one) * clipped
    seconds_new = beta_two * seconds + (1.0 - beta_two) * clipped * clipped
    direction = (
        moments_new
        / (1.0 - beta_one**STEP)
        / (jnp.sqrt(seconds_new / (1.0 - beta_two**STEP)) + adam_eps)
    )
    params_new = params - learning_rate * (direction + weight_decay * params)
    return (params_new, moments_new, seconds_new)


def advance(stream, branch, current, col_first, col_count):
    if current + 1 < LAYERS:
        widened = lax.all_gather(branch, "fsdp", axis=1, tiled=True)
        return stream + widened.astype(jnp.float32)
    return lax.dynamic_slice_in_dim(stream, col_first, col_count, 1) + branch.astype(jnp.float32)


def per_device(
    tokens, counts, patch_index, clip_limit, norm_gain, params, moments, seconds, gradients
):
    squares = lax.psum(jnp.sum(gradients * gradients), ("dp", "fsdp"))
    factor = jnp.minimum(1.0, clip_limit / (jnp.sqrt(squares) + 1e-06))
    params_new, moments_new, seconds_new = adam_update(params, moments, seconds, gradients, factor)
    weights = params_new.astype(jnp.bfloat16)
    tok_rows = tokens.shape[0]
    col_count = weights.shape[2]
    col_first = lax.axis_index("fsdp") * col_count
    valid = lax.broadcasted_iota(jnp.int32, (tok_rows, 1), 0) < counts[0]
    stream = jnp.where(valid, tokens.astype(jnp.float32) + position_code(patch_index), 0.0)
    gathered = lax.all_gather(weights, "dp", axis=1, tiled=True)
    for current in range(LAYERS):
        normed = layer_norm(stream, norm_gain[current])
        branch = jnp.dot(normed, gathered[current], preferred_element_type=jnp.float32).astype(
            jnp.bfloat16
        )
        stream = advance(stream, branch, current, col_first, col_count)
    mixed = jnp.where(valid, stream, 0.0).astype(jnp.bfloat16)
    return (params_new, moments_new, seconds_new, mixed)


def solution(mesh):
    in_specs = (
        P("dp", None),
        P("dp"),
        P("dp"),
        P(),
        P(),
        P(None, "dp", "fsdp"),
        P(None, "dp", "fsdp"),
        P(None, "dp", "fsdp"),
        P(None, "dp", "fsdp"),
    )
    out_specs = (
        P(None, "dp", "fsdp"),
        P(None, "dp", "fsdp"),
        P(None, "dp", "fsdp"),
        P("dp", "fsdp"),
    )
    return jax.shard_map(
        per_device, mesh=mesh, in_specs=in_specs, out_specs=out_specs, check_vma=False
    )
```

profile of v0, /device:TPU:0, one launch (start us, length us, event | category | flops | bytes accessed | tf_op | source)
XLA Modules:
  0.0 556.9 jit_solution(18285389573598532073)
XLA Ops:
  7.2 0.0 all-gather.5.cloned.1.call-start
  7.2 6.1 %multiply_reduce_fusion.4 = f32[]{:T(128)} fusion(f32[4,512,1024]{2,1,0:T(8,128)} %param.17), kind=kLoop, calls=%fused_computation.25 | loop fusion | flops 4194303 | bytes 8388612 | tf_op jit(solution)/shard_map/reduce_sum | solution.py:58
  14.0 42.2 %psum.7 = f32[]{:T(128)} all-reduce(f32[]{:T(128)} %multiply_reduce_fusion.4), channel_id=1, replica_groups=mesh['dp'=8,'fsdp'=4] {'dp','fsdp'}, use_global_device_ids=true, to_apply=%region_1.0 | all-reduce | flops 1 | bytes 8 | tf_op jit(solution)/shard_map/psum | solution.py:58
  57.0 0.0 copy-start.5
  57.0 20.8 %fusion.30 = (bf16[4,512,1024]{2,1,0:T(8,128)(2,1)}, f32[4,512,1024]{2,1,0:T(8,128)}, f32[4,512,1024]{2,1,0:T(8,128)}, f32[4,512,1024]{2,1,0:T(8,128)}) fusion(f32[4,512,1024]{2,1,0:T(8,128)} %param.14, f32[4,512,1024]{2,1,0:T(8,128)} %param.17, f32[]{:T(128)S(6)} %min.3, f32[4,512,1024]{2,1,0:T(8,128)} %param.15, f32[4,512,1024]{2,1,0:T(8,128)} %param.16), kind=kLoop, calls=%fused_computation.71 | loop fusion | flops 35651584 | bytes 62914564 | tf_op jit(solution)/shard_map/convert_element_type | solution.py:61
  77.8 0.0 all-gather.5.cloned.1.call-update
  77.8 0.2 all-gather.7.cloned.1.call-start
  78.0 0.0 copy-start.3
  78.9 0.0 copy-done.5
  78.9 14.7 %multiply_sine_fusion.1 = (f32[512,1024]{1,0:T(8,128)S(1)}, f32[512,1024]{1,0:T(8,128)S(1)}, f32[512,1024]{1,0:T(8,128)S(1)}, f32[512,1024]{1,0:T(8,128)S(1)}) fusion(f32[1024]{0:T(1024)S(1)} %negate_power_fusion, f32[512]{0:T(512)S(1)} %get-tuple-element.24, f32[512]{0:T(512)S(1)} %get-tuple-element.25), kind=kLoop, calls=%fused_computation.41 | loop fusion | flops 1048576 | bytes 8396800 | tf_op jit(solution)/shard_map/sin | solution.py:24
  93.7 0.0 copy-done.3
  93.7 1.7 fusion.28
  95.4 0.0 copy-start
  95.4 0.0 copy-start.4
  95.4 3.2 copy-done
  98.6 1.0 multiply_reduce_fusion.3
  99.6 0.0 copy-done.4
  99.6 139.0 %all-gather.5.cloned.1.call-done = bf16[4,4096,1024]{2,1,0:T(8,128)(2,1)} async-done(((bf16[4,512,1024]{2,1,0:T(8,128)(2,1)}), bf16[4,4096,1024]{2,1,0:T(8,128)(2,1)}) %all-gather.5.cloned.1.call-update) | async-done | bytes 33554448 | tf_op jit(solution)/shard_map/all_gather | solution.py:67
  238.6 11.3 %fusion.18 = bf16[512,1024]{1,0:T(8,128)(2,1)} fusion(bf16[4,4096,1024]{2,1,0:T(8,128)(2,1)} %all-gather.5.cloned.1.call-done, f32[512,4096]{1,0:T(8,128)} %copy-done, f32[4096]{0:T(1024)S(1)} %bitcast.33, f32[512]{0:T(512)S(1)} %add_rsqrt_fusion.3, f32[512]{0:T(512)S(1)} %broadcast_multiply_fusion.3), kind=kOutput, calls=%fused_computation.43 | convolution fusion | flops 4303880192 | bytes 17846272 | tf_op jit(solution)/shard_map/dot_general | solution.py:70
  249.9 0.0 all-gather.7.cloned.1.call-update
  249.9 0.0 all-gather.9.cloned.1.call-start
  250.0 80.8 %all-gather.7.cloned.1.call-done = bf16[512,4096]{1,0:T(8,128)(2,1)} async-done(((bf16[512,1024]{1,0:T(8,128)(2,1)}), bf16[512,4096]{1,0:T(8,128)(2,1)}) %all-gather.7.cloned.1.call-update) | async-done | bytes 4194320 | tf_op jit(solution)/shard_map/all_gather | solution.py:50
  330.8 0.0 copy-start.2
  330.8 0.0 slice-start
  330.8 5.6 %fusion.22 = f32[512]{0:T(512)S(1)} fusion(f32[512,4096]{1,0:T(8,128)} %copy-done, bf16[512,4096]{1,0:T(8,128)(2,1)} %all-gather.7.cloned.1.call-done), kind=kLoop, calls=%fused_computation.47 | loop fusion | flops 6290944 | bytes 12584960 | tf_op jit(solution)/shard_map/reduce_sum | solution.py:29
  336.4 0.1 copy-done.2
  336.6 0.0 slice-start.1
  336.6 5.2 multiply_reduce_fusion.2
  341.8 0.0 slice-done
  341.8 0.0 slice-done.1
  341.8 9.2 %fusion.19 = bf16[512,1024]{1,0:T(8,128)(2,1)} fusion(bf16[4,4096,1024]{2,1,0:T(8,128)(2,1)} %all-gather.5.cloned.1.call-done, f32[4096]{0:T(1024)S(1)} %bitcast.32, f32[512]{0:T(512)S(1)} %add_rsqrt_fusion.2, f32[512]{0:T(512)S(1)} %broadcast_multiply_fusion.2, f32[512,4096]{1,0:T(8,128)S(1)} %bitcast.29, bf16[512,4096]{1,0:T(8,128)(2,1)S(1)} %copy-done.2), kind=kOutput, calls=%fused_computation.44 | convolution fusion | flops 4308074496 | bytes 22040576 | tf_op jit(solution)/shard_map/dot_general | solution.py:70
  351.0 0.0 all-gather.9.cloned.1.call-update
  351.1 0.3 all-gather.11.cloned.1.call-start
  351.4 79.1 %all-gather.9.cloned.1.call-done = bf16[512,4096]{1,0:T(8,128)(2,1)} async-done(((bf16[512,1024]{1,0:T(8,128)(2,1)}), bf16[512,4096]{1,0:T(8,128)(2,1)}) %all-gather.9.cloned.1.call-update) | async-done | bytes 4194320 | tf_op jit(solution)/shard_map/all_gather | solution.py:50
  430.4 10.3 %fusion.27 = (f32[512]{0:T(512)S(1)}, f32[512,4096]{1,0:T(8,128)}) fusion(bf16[512,4096]{1,0:T(8,128)(2,1)} %all-gather.9.cloned.1.call-done, f32[512,4096]{1,0:T(8,128)} %copy-done, bf16[512,4096]{1,0:T(8,128)(2,1)} %all-gather.7.cloned.1.call-done), kind=kLoop, calls=%fused_computation.69 | loop fusion | flops 10485248 | bytes 25167872 | tf_op jit(solution)/shard_map/reduce_sum | solution.py:29
  440.7 0.0 copy-start.1
  440.8 4.5 multiply_reduce_fusion.1
  445.3 1.3 copy-done.1
  446.5 9.0 %fusion.20 = bf16[512,1024]{1,0:T(8,128)(2,1)} fusion(bf16[4,4096,1024]{2,1,0:T(8,128)(2,1)} %all-gather.5.cloned.1.call-done, f32[512,4096]{1,0:T(8,128)S(1)} %copy-done.1, f32[4096]{0:T(1024)S(1)} %bitcast.31, f32[512]{0:T(512)S(1)} %add_rsqrt_fusion.1, f32[512]{0:T(512)S(1)} %broadcast_multiply_fusion.1), kind=kOutput, calls=%fused_computation.45 | convolution fusion | flops 4303880192 | bytes 17846272 | tf_op jit(solution)/shard_map/dot_general | solution.py:70
  455.6 0.0 all-gather.11.cloned.1.call-update
  455.6 79.4 %all-gather.11.cloned.1.call-done = bf16[512,4096]{1,0:T(8,128)(2,1)} async-done(((bf16[512,1024]{1,0:T(8,128)(2,1)}), bf16[512,4096]{1,0:T(8,128)(2,1)}) %all-gather.11.cloned.1.call-update) | async-done | bytes 4194320 | tf_op jit(solution)/shard_map/all_gather | solution.py:50
  535.0 5.5 fusion.26
  540.5 1.0 multiply_reduce_fusion
  541.4 8.9 %select_convert_fusion = bf16[512,1024]{1,0:T(8,128)(2,1)} fusion(f32[512,4096]{1,0:T(8,128)S(1)} %get-tuple-element.5, s32[]{:T(128)S(6)} %select_n.26, bf16[4,4096,1024]{2,1,0:T(8,128)(2,1)} %all-gather.5.cloned.1.call-done, f32[4096]{0:T(1024)S(1)} %bitcast.30, f32[512]{0:T(512)S(1)} %add_rsqrt_fusion, f32[512]{0:T(512)S(1)} %broadcast_multiply_fusion, ...), kind=kOutput, calls=%fused_computation.42 | convolution fusion | flops 4305977344 | bytes 19943940 | tf_op jit(solution)/shard_map/dot_general | solution.py:70
  (13 shorter events, 0.1 us)
Async XLA Ops:
  7.2 231.5 %all-gather.5.cloned.1.call-start = ((), (), s32[]{:S(2)}) async-start(), calls=%async_computation | async-start | bytes 37748736 | tf_op jit(solution)/shard_map/all_gather | solution.py:67
  57.0 21.9 %copy-start.5 = (s32[512]{0:T(512)S(1)}, s32[512]{0:T(512)}, u32[]{:S(2)}) copy-start(s32[512]{0:T(512)} %param.11) | copy-start | bytes 6148
  77.8 253.0 %all-gather.7.cloned.1.call-start = ((), (), s32[]{:S(2)}) async-start(), calls=%async_computation.1 | async-start | bytes 5242880 | tf_op jit(solution)/shard_map/all_gather | solution.py:50
  78.0 15.6 %copy-start.3 = (bf16[512,4096]{1,0:T(8,128)(2,1)S(1)}, bf16[512,4096]{1,0:T(8,128)(2,1)}, u32[]{:S(2)}) copy-start(bf16[512,4096]{1,0:T(8,128)(2,1)} %param.9) | copy-start | bytes 12582916
  95.4 3.2 copy-start
  95.4 4.2 copy-start.4
  249.9 180.5 %all-gather.9.cloned.1.call-start = ((), (), s32[]{:S(2)}) async-start(), calls=%async_computation.2 | async-start | bytes 5242880 | tf_op jit(solution)/shard_map/all_gather | solution.py:50
  330.8 5.8 %copy-start.2 = (bf16[512,4096]{1,0:T(8,128)(2,1)S(1)}, bf16[512,4096]{1,0:T(8,128)(2,1)}, u32[]{:S(2)}) copy-start(bf16[512,4096]{1,0:T(8,128)(2,1)} %all-gather.7.cloned.1.call-done) | copy-start | bytes 12582916
  330.8 11.0 %slice-start = ((s8[8388608]{0:T(1024)(128)(4,1)}), s8[4194304]{0:T(1024)(128)(4,1)S(1)}, s32[]{:S(2)}) async-start(s8[8388608]{0:T(1024)(128)(4,1)} %bitcast.28), calls=%async_computation.4 | async-start | bytes 8388608
  336.6 5.2 slice-start.1
  351.1 183.9 %all-gather.11.cloned.1.call-start = ((), (), s32[]{:S(2)}) async-start(), calls=%async_computation.3 | async-start | bytes 5242880 | tf_op jit(solution)/shard_map/all_gather | solution.py:50
  440.7 5.8 %copy-start.1 = (f32[512,4096]{1,0:T(8,128)S(1)}, f32[512,4096]{1,0:T(8,128)}, u32[]{:S(2)}) copy-start(f32[512,4096]{1,0:T(8,128)} %get-tuple-element.7) | copy-start | bytes 25165828
Sparse Core Ops, SparseCore 0:
  77.9 160.6 all-gather.4
  250.0 80.7 all-gather.6
  351.2 79.2 all-gather.8
  455.7 79.2 all-gather.10
where the time goes:
time: 557 us
  waiting for transfers between devices  378 us (68%)
  other arithmetic  76.5 us (14%)
  blocking collectives  42.2 us (8%)
  matrix products  38.4 us (7%)
  between operations  16.1 us (3%)
    all_gather x3, waiting for transfers between devices, advance(): widened = lax.all_gather(branch, 'fsdp', axis=1, tiled=True)  239 us
    all_gather x1, waiting for transfers between devices, per_device(): gathered = lax.all_gather(weights, 'dp', axis=1, tiled=True)  139 us
    psum x1, blocking collectives, per_device(): squares = lax.psum(jnp.sum(gradients * gradients), ('dp', 'fsdp'))  42.2 us
    dot_general x4, matrix products, per_device(): jnp.dot(normed, gathered[current], preferred_element_type=jnp.float32)  38.4 us
    reduce_sum x4, other arithmetic, layer_norm(): centre = jnp.mean(stream, axis=1, keepdims=True)  23.1 us
    convert_element_type x1, other arithmetic, per_device(): weights = params_new.astype(jnp.bfloat16)  20.8 us
    sin x1, other arithmetic, position_code(): jnp.sin(across)  14.7 us
    reduce_sum x4, other arithmetic, layer_norm(): spread = jnp.mean(shifted * shifted, axis=1, keepdims=True)  11.6 us
  transfers between devices with their start and end apart: 4, of which 4 were waited for; matrix products, arithmetic and copies ran while one was open for 3% of the time, Pallas kernels for 0%

commit v1 on v0

--- a/solution.py
+++ b/solution.py
@@ -47,7 +47,14 @@
 
 def advance(stream, branch, current, col_first, col_count):
     if current + 1 < LAYERS:
-        widened = lax.all_gather(branch, "fsdp", axis=1, tiled=True)
+        ring = [branch]
+        for hop in range(3):
+            ring.append(lax.ppermute(ring[-1], "fsdp", [(dev, (dev + 1) % 4) for dev in range(4)]))
+        widened = jnp.roll(
+            jnp.concatenate(ring[::-1], axis=1),
+            (lax.axis_index("fsdp") + 1) * ring[0].shape[1],
+            axis=1,
+        )
         return stream + widened.astype(jnp.float32)
     return lax.dynamic_slice_in_dim(stream, col_first, col_count, 1) + branch.astype(jnp.float32)
 

time: 557 us -> 537 us (0.964); the launches traced: 557 us -> 528 us
  waiting for transfers between devices: 378 us -> 354 us
    all_gather x3 -> x0, waiting for transfers between devices: 239 us -> none  [advance(): widened = lax.all_gather(branch, 'fsdp', axis=1, tiled=True)]
    ppermute x0 -> x9, waiting for transfers between devices: none -> 215 us  [advance(): lax.ppermute(ring[-1], 'fsdp', [(dev, (dev + 1) % 4) for dev in range(4)])]
    reduce_sum x4, other arithmetic: 11.6 us -> 3.87 us  [layer_norm(): spread = jnp.mean(shifted * shifted, axis=1, keepdims=True)]
  transfers between devices with their start and end apart: 4 -> 10, of which waited for: 4 -> 10; matrix products, arithmetic and copies ran while one was open for 3% -> 3% of each run, Pallas kernels for 0% -> 0%
where the time goes in v1:
time: 537 us; the launch traced here: 528 us
  waiting for transfers between devices  354 us (66%)
  other arithmetic  72.1 us (13%)
  blocking collectives  42.2 us (8%)
  matrix products  37.7 us (7%)
  between operations  16.7 us (3%)
    ppermute x9, waiting for transfers between devices, advance(): lax.ppermute(ring[-1], 'fsdp', [(dev, (dev + 1) % 4) for dev in range(4)])  215 us
    all_gather x1, waiting for transfers between devices, per_device(): gathered = lax.all_gather(weights, 'dp', axis=1, tiled=True)  139 us
    psum x1, blocking collectives, per_device(): squares = lax.psum(jnp.sum(gradients * gradients), ('dp', 'fsdp'))  42.2 us
    dot_general x4, matrix products, per_device(): jnp.dot(normed, gathered[current], preferred_element_type=jnp.float32)  37.7 us
    reduce_sum x4, other arithmetic, layer_norm(): centre = jnp.mean(stream, axis=1, keepdims=True)  26.4 us
    convert_element_type x1, other arithmetic, per_device(): weights = params_new.astype(jnp.bfloat16)  20.8 us
    sin x1, other arithmetic, position_code(): jnp.sin(across)  14.7 us
  transfers between devices with their start and end apart: 10, of which 10 were waited for; matrix products, arithmetic and copies ran while one was open for 3% of the time, Pallas kernels for 0%

profile of v1, /device:TPU:0, one launch (start us, length us, event | category | flops | bytes accessed | tf_op | source)
XLA Modules:
  0.0 528.1 jit_solution(17007816327913139336)
XLA Ops:
  7.2 0.0 all-gather.2.cloned.1.call-start
  7.2 6.1 %multiply_reduce_fusion.4 = f32[]{:T(128)} fusion(f32[4,512,1024]{2,1,0:T(8,128)} %param.19), kind=kLoop, calls=%fused_computation.49 | loop fusion | flops 4194303 | bytes 8388612 | tf_op jit(solution)/shard_map/reduce_sum | solution.py:65
  14.0 42.2 %psum.7 = f32[]{:T(128)} all-reduce(f32[]{:T(128)} %multiply_reduce_fusion.4), channel_id=1, replica_groups=mesh['dp'=8,'fsdp'=4] {'dp','fsdp'}, use_global_device_ids=true, to_apply=%region_1.0 | all-reduce | flops 1 | bytes 8 | tf_op jit(solution)/shard_map/psum | solution.py:65
  57.0 0.0 copy-start.5
  57.0 20.8 %fusion.51 = (bf16[4,512,1024]{2,1,0:T(8,128)(2,1)}, f32[4,512,1024]{2,1,0:T(8,128)}, f32[4,512,1024]{2,1,0:T(8,128)}, f32[4,512,1024]{2,1,0:T(8,128)}) fusion(f32[4,512,1024]{2,1,0:T(8,128)} %param.16, f32[4,512,1024]{2,1,0:T(8,128)} %param.19, f32[]{:T(128)S(6)} %min.3, f32[4,512,1024]{2,1,0:T(8,128)} %param.17, f32[4,512,1024]{2,1,0:T(8,128)} %param.18), kind=kLoop, calls=%fused_computation.116 | loop fusion | flops 35651584 | bytes 62914564 | tf_op jit(solution)/shard_map/convert_element_type | solution.py:68
  77.8 0.0 all-gather.2.cloned.1.call-update
  77.8 0.0 copy-start.2
  78.6 0.0 copy-done.5
  78.7 14.7 %multiply_sine_fusion.1 = (f32[512,1024]{1,0:T(8,128)S(1)}, f32[512,1024]{1,0:T(8,128)S(1)}, f32[512,1024]{1,0:T(8,128)S(1)}, f32[512,1024]{1,0:T(8,128)S(1)}) fusion(f32[1024]{0:T(1024)S(1)} %negate_power_fusion, f32[512]{0:T(512)S(1)} %get-tuple-element.27, f32[512]{0:T(512)S(1)} %get-tuple-element.28), kind=kLoop, calls=%fused_computation.86 | loop fusion | flops 1048576 | bytes 8396800 | tf_op jit(solution)/shard_map/sin | solution.py:24
  93.4 0.0 copy-done.2
  93.4 2.0 fusion.49
  95.4 0.0 copy-start
  95.4 0.0 copy-start.4
  95.4 3.2 copy-done
  98.6 1.0 multiply_reduce_fusion.3
  99.6 0.0 copy-done.4
  99.6 139.0 %all-gather.2.cloned.1.call-done = bf16[4,4096,1024]{2,1,0:T(8,128)(2,1)} async-done(((bf16[4,512,1024]{2,1,0:T(8,128)(2,1)}), bf16[4,4096,1024]{2,1,0:T(8,128)(2,1)}) %all-gather.2.cloned.1.call-update) | async-done | bytes 33554448 | tf_op jit(solution)/shard_map/all_gather | solution.py:74
  238.6 10.3 %fusion.39 = bf16[512,1024]{1,0:T(8,128)(2,1)S(1)} fusion(bf16[4,4096,1024]{2,1,0:T(8,128)(2,1)} %all-gather.2.cloned.1.call-done, f32[512,4096]{1,0:T(8,128)} %copy-done, f32[4096]{0:T(1024)S(1)} %bitcast.31, f32[512]{0:T(512)S(1)} %add_rsqrt_fusion.3, f32[512]{0:T(512)S(1)} %broadcast_multiply_fusion.3), kind=kOutput, calls=%fused_computation.88 | convolution fusion | flops 4303880192 | bytes 17846272 | tf_op jit(solution)/shard_map/dot_general | solution.py:77
  248.9 1.5 collective-permute-start
  250.5 25.6 %collective-permute-done = bf16[512,1024]{1,0:T(8,128)(2,1)S(1)} collective-permute-done((bf16[512,1024]{1,0:T(8,128)(2,1)S(1)}, bf16[512,1024]{1,0:T(8,128)(2,1)S(1)}, u32[]{:S(2)}, u32[]{:S(2)}) %collective-permute-start) | collective-permute-done | bytes 1048608 | tf_op jit(solution)/shard_map/ppermute | solution.py:52
  276.1 0.0 collective-permute-start.1
  276.1 26.2 %collective-permute-done.1 = bf16[512,1024]{1,0:T(8,128)(2,1)S(1)} collective-permute-done((bf16[512,1024]{1,0:T(8,128)(2,1)S(1)}, bf16[512,1024]{1,0:T(8,128)(2,1)S(1)}, u32[]{:S(2)}, u32[]{:S(2)}) %collective-permute-start.1) | collective-permute-done | bytes 1048608 | tf_op jit(solution)/shard_map/ppermute | solution.py:52
  302.4 0.0 collective-permute-start.2
  302.4 25.5 %collective-permute-done.2 = bf16[512,1024]{1,0:T(8,128)(2,1)} collective-permute-done((bf16[512,1024]{1,0:T(8,128)(2,1)S(1)}, bf16[512,1024]{1,0:T(8,128)(2,1)}, u32[]{:S(2)}, u32[]{:S(2)}) %collective-permute-start.2) | collective-permute-done | bytes 1048608 | tf_op jit(solution)/shard_map/ppermute | solution.py:52
  327.9 8.8 %fusion.48 = (f32[512]{0:T(512)S(1)}, f32[512,4096]{1,0:T(8,128)S(1)}) fusion(f32[512,4096]{1,0:T(8,128)} %copy-done, s32[]{:T(128)S(6)} %select_n.42, bf16[512,1024]{1,0:T(8,128)(2,1)S(1)} %fusion.39, bf16[512,1024]{1,0:T(8,128)(2,1)S(1)} %collective-permute-done, bf16[512,1024]{1,0:T(8,128)(2,1)S(1)} %collective-permute-done.1, ...), kind=kLoop, calls=%fused_computation.114 | loop fusion | flops 37748224 | bytes 20973572 | tf_op jit(solution)/shard_map/reduce_sum | solution.py:29
  336.7 1.0 multiply_reduce_fusion.2
  337.7 8.1 %fusion.40 = bf16[512,1024]{1,0:T(8,128)(2,1)S(1)} fusion(bf16[4,4096,1024]{2,1,0:T(8,128)(2,1)} %all-gather.2.cloned.1.call-done, f32[512,4096]{1,0:T(8,128)S(1)} %get-tuple-element.10, f32[4096]{0:T(1024)S(1)} %bitcast.30, f32[512]{0:T(512)S(1)} %add_rsqrt_fusion.2, f32[512]{0:T(512)S(1)} %broadcast_multiply_fusion.2), kind=kOutput, calls=%fused_computation.89 | convolution fusion | flops 4303880192 | bytes 17846272 | tf_op jit(solution)/shard_map/dot_general | solution.py:77
  345.8 0.1 collective-permute-start.3
  345.9 24.5 %collective-permute-done.3 = bf16[512,1024]{1,0:T(8,128)(2,1)S(1)} collective-permute-done((bf16[512,1024]{1,0:T(8,128)(2,1)S(1)}, bf16[512,1024]{1,0:T(8,128)(2,1)S(1)}, u32[]{:S(2)}, u32[]{:S(2)}) %collective-permute-start.3) | collective-permute-done | bytes 1048608 | tf_op jit(solution)/shard_map/ppermute | solution.py:52
  370.4 0.0 collective-permute-start.4
  370.4 23.7 %collective-permute-done.4 = bf16[512,1024]{1,0:T(8,128)(2,1)S(1)} collective-permute-done((bf16[512,1024]{1,0:T(8,128)(2,1)S(1)}, bf16[512,1024]{1,0:T(8,128)(2,1)S(1)}, u32[]{:S(2)}, u32[]{:S(2)}) %collective-permute-start.4) | collective-permute-done | bytes 1048608 | tf_op jit(solution)/shard_map/ppermute | solution.py:52
  394.1 0.0 collective-permute-start.5
  394.1 1.0 copy-done.3
  395.1 22.0 %collective-permute-done.5 = bf16[512,1024]{1,0:T(8,128)(2,1)} collective-permute-done((bf16[512,1024]{1,0:T(8,128)(2,1)S(1)}, bf16[512,1024]{1,0:T(8,128)(2,1)}, u32[]{:S(2)}, u32[]{:S(2)}) %collective-permute-start.5) | collective-permute-done | bytes 1048608 | tf_op jit(solution)/shard_map/ppermute | solution.py:52
  417.1 7.5 %fusion.47 = (f32[512]{0:T(512)S(1)}, f32[512,4096]{1,0:T(8,128)S(1)}) fusion(f32[512,4096]{1,0:T(8,128)S(1)} %get-tuple-element.10, s32[]{:T(128)S(6)} %select_n.42, bf16[512,1024]{1,0:T(8,128)(2,1)S(1)} %fusion.40, bf16[512,1024]{1,0:T(8,128)(2,1)S(1)} %collective-permute-done.3, bf16[512,1024]{1,0:T(8,128)(2,1)} %copy-done.3, ...), kind=kLoop, calls=%fused_computation.113 | loop fusion | flops 37748224 | bytes 20973572 | tf_op jit(solution)/shard_map/reduce_sum | solution.py:29
  424.5 0.0 copy-start.1
  424.5 1.0 multiply_reduce_fusion.1
  425.5 10.1 %fusion.41 = bf16[512,1024]{1,0:T(8,128)(2,1)S(1)} fusion(bf16[4,4096,1024]{2,1,0:T(8,128)(2,1)} %all-gather.2.cloned.1.call-done, f32[512,4096]{1,0:T(8,128)S(1)} %get-tuple-element.8, f32[4096]{0:T(1024)S(1)} %bitcast.29, f32[512]{0:T(512)S(1)} %add_rsqrt_fusion.1, f32[512]{0:T(512)S(1)} %broadcast_multiply_fusion.1), kind=kOutput, calls=%fused_computation.90 | convolution fusion | flops 4303880192 | bytes 17846272 | tf_op jit(solution)/shard_map/dot_general | solution.py:77
  435.6 0.0 copy-done.1
  435.6 0.1 collective-permute-start.6
  435.7 23.3 %collective-permute-done.6 = bf16[512,1024]{1,0:T(8,128)(2,1)S(1)} collective-permute-done((bf16[512,1024]{1,0:T(8,128)(2,1)S(1)}, bf16[512,1024]{1,0:T(8,128)(2,1)S(1)}, u32[]{:S(2)}, u32[]{:S(2)}) %collective-permute-start.6) | collective-permute-done | bytes 1048608 | tf_op jit(solution)/shard_map/ppermute | solution.py:52
  459.0 0.0 collective-permute-start.7
  459.0 23.1 %collective-permute-done.7 = bf16[512,1024]{1,0:T(8,128)(2,1)} collective-permute-done((bf16[512,1024]{1,0:T(8,128)(2,1)S(1)}, bf16[512,1024]{1,0:T(8,128)(2,1)}, u32[]{:S(2)}, u32[]{:S(2)}) %collective-permute-start.7) | collective-permute-done | bytes 1048608 | tf_op jit(solution)/shard_map/ppermute | solution.py:52
  482.1 0.0 collective-permute-start.8
  482.1 20.6 %collective-permute-done.8 = bf16[512,1024]{1,0:T(8,128)(2,1)} collective-permute-done((bf16[512,1024]{1,0:T(8,128)(2,1)}, bf16[512,1024]{1,0:T(8,128)(2,1)}, u32[]{:S(2)}, u32[]{:S(2)}) %collective-permute-start.8) | collective-permute-done | bytes 1048608 | tf_op jit(solution)/shard_map/ppermute | solution.py:52
  502.7 8.2 %fusion.46 = (f32[512]{0:T(512)S(1)}, f32[512,4096]{1,0:T(8,128)S(1)}) fusion(f32[512,4096]{1,0:T(8,128)} %copy-done.1, s32[]{:T(128)S(6)} %select_n.42, bf16[512,1024]{1,0:T(8,128)(2,1)S(1)} %fusion.41, bf16[512,1024]{1,0:T(8,128)(2,1)S(1)} %collective-permute-done.6, bf16[512,1024]{1,0:T(8,128)(2,1)} %collective-permute-done.7, ...), kind=kLoop, calls=%fused_computation.112 | loop fusion | flops 37748224 | bytes 20973572 | tf_op jit(solution)/shard_map/reduce_sum | solution.py:29
  510.9 1.0 multiply_reduce_fusion
  511.8 9.1 %select_convert_fusion = bf16[512,1024]{1,0:T(8,128)(2,1)} fusion(f32[512,4096]{1,0:T(8,128)S(1)} %get-tuple-element.6, s32[]{:T(128)S(6)} %select_n.35, bf16[4,4096,1024]{2,1,0:T(8,128)(2,1)} %all-gather.2.cloned.1.call-done, f32[4096]{0:T(1024)S(1)} %bitcast.28, f32[512]{0:T(512)S(1)} %add_rsqrt_fusion, f32[512]{0:T(512)S(1)} %broadcast_multiply_fusion, ...), kind=kOutput, calls=%fused_computation.87 | convolution fusion | flops 4305977344 | bytes 19943940 | tf_op jit(solution)/shard_map/dot_general | solution.py:77
  (13 shorter events, 0.1 us)
Async XLA Ops:
  7.2 231.5 %all-gather.2.cloned.1.call-start = ((), (), s32[]{:S(2)}) async-start(), calls=%async_computation | async-start | bytes 37748736 | tf_op jit(solution)/shard_map/all_gather | solution.py:74
  57.0 21.7 %copy-start.5 = (s32[512]{0:T(512)S(1)}, s32[512]{0:T(512)}, u32[]{:S(2)}) copy-start(s32[512]{0:T(512)} %param.13) | copy-start | bytes 6148
  77.8 15.6 %copy-start.2 = (bf16[512,4096]{1,0:T(8,128)(2,1)S(1)}, bf16[512,4096]{1,0:T(8,128)(2,1)}, u32[]{:S(2)}) copy-start(bf16[512,4096]{1,0:T(8,128)(2,1)} %param.11) | copy-start | bytes 12582916
  95.4 3.2 copy-start
  95.4 4.2 copy-start.4
  248.9 27.2 %collective-permute-start = (bf16[512,1024]{1,0:T(8,128)(2,1)S(1)}, bf16[512,1024]{1,0:T(8,128)(2,1)S(1)}, u32[]{:S(2)}, u32[]{:S(2)}) collective-permute-start(bf16[512,1024]{1,0:T(8,128)(2,1)S(1)} %fusion.39), channel_id=1, source_target_pairs={{0,1},{1,2},{2,3},{3,0},{4,5},{5,6},{6,7},{7,4},{8,9},{9,10},{10,1... | collective-permute-start | bytes 3145736 | tf_op jit(solution)/shard_map/ppermute | solution.py:52
  276.1 26.3 %collective-permute-start.1 = (bf16[512,1024]{1,0:T(8,128)(2,1)S(1)}, bf16[512,1024]{1,0:T(8,128)(2,1)S(1)}, u32[]{:S(2)}, u32[]{:S(2)}) collective-permute-start(bf16[512,1024]{1,0:T(8,128)(2,1)S(1)} %collective-permute-done), channel_id=1, source_target_pairs={{0,1},{1,2},{2,3},{3,0},{4,5},{5,6},{6,7},{7,4},{8,9},{9,10},{10,1... | collective-permute-start | bytes 3145736 | tf_op jit(solution)/shard_map/ppermute | solution.py:52
  302.4 25.5 %collective-permute-start.2 = (bf16[512,1024]{1,0:T(8,128)(2,1)S(1)}, bf16[512,1024]{1,0:T(8,128)(2,1)}, u32[]{:S(2)}, u32[]{:S(2)}) collective-permute-start(bf16[512,1024]{1,0:T(8,128)(2,1)S(1)} %collective-permute-done.1), channel_id=1, source_target_pairs={{0,1},{1,2},{2,3},{3,0},{4,5},{5,6},{6,7},{7,4},{8,9},{9,10},{10,1... | collective-permute-start | bytes 3145736 | tf_op jit(solution)/shard_map/ppermute | solution.py:52
  345.8 24.6 %collective-permute-start.3 = (bf16[512,1024]{1,0:T(8,128)(2,1)S(1)}, bf16[512,1024]{1,0:T(8,128)(2,1)S(1)}, u32[]{:S(2)}, u32[]{:S(2)}) collective-permute-start(bf16[512,1024]{1,0:T(8,128)(2,1)S(1)} %fusion.40), channel_id=1, source_target_pairs={{0,1},{1,2},{2,3},{3,0},{4,5},{5,6},{6,7},{7,4},{8,9},{9,10},{10,1... | collective-permute-start | bytes 3145736 | tf_op jit(solution)/shard_map/ppermute | solution.py:52
  370.4 23.7 %collective-permute-start.4 = (bf16[512,1024]{1,0:T(8,128)(2,1)S(1)}, bf16[512,1024]{1,0:T(8,128)(2,1)S(1)}, u32[]{:S(2)}, u32[]{:S(2)}) collective-permute-start(bf16[512,1024]{1,0:T(8,128)(2,1)S(1)} %collective-permute-done.3), channel_id=1, source_target_pairs={{0,1},{1,2},{2,3},{3,0},{4,5},{5,6},{6,7},{7,4},{8,9},{9,10},{10,1... | collective-permute-start | bytes 3145736 | tf_op jit(solution)/shard_map/ppermute | solution.py:52
  394.1 1.0 copy-start.3
  394.1 22.9 %collective-permute-start.5 = (bf16[512,1024]{1,0:T(8,128)(2,1)S(1)}, bf16[512,1024]{1,0:T(8,128)(2,1)}, u32[]{:S(2)}, u32[]{:S(2)}) collective-permute-start(bf16[512,1024]{1,0:T(8,128)(2,1)S(1)} %collective-permute-done.4), channel_id=1, source_target_pairs={{0,1},{1,2},{2,3},{3,0},{4,5},{5,6},{6,7},{7,4},{8,9},{9,10},{10,1... | collective-permute-start | bytes 3145736 | tf_op jit(solution)/shard_map/ppermute | solution.py:52
  424.5 11.1 %copy-start.1 = (f32[512,4096]{1,0:T(8,128)}, f32[512,4096]{1,0:T(8,128)S(1)}, u32[]{:S(2)}) copy-start(f32[512,4096]{1,0:T(8,128)S(1)} %get-tuple-element.8) | copy-start | bytes 25165828
  435.6 23.4 %collective-permute-start.6 = (bf16[512,1024]{1,0:T(8,128)(2,1)S(1)}, bf16[512,1024]{1,0:T(8,128)(2,1)S(1)}, u32[]{:S(2)}, u32[]{:S(2)}) collective-permute-start(bf16[512,1024]{1,0:T(8,128)(2,1)S(1)} %fusion.41), channel_id=1, source_target_pairs={{0,1},{1,2},{2,3},{3,0},{4,5},{5,6},{6,7},{7,4},{8,9},{9,10},{10,1... | collective-permute-start | bytes 3145736 | tf_op jit(solution)/shard_map/ppermute | solution.py:52
  459.0 23.1 %collective-permute-start.7 = (bf16[512,1024]{1,0:T(8,128)(2,1)S(1)}, bf16[512,1024]{1,0:T(8,128)(2,1)}, u32[]{:S(2)}, u32[]{:S(2)}) collective-permute-start(bf16[512,1024]{1,0:T(8,128)(2,1)S(1)} %collective-permute-done.6), channel_id=1, source_target_pairs={{0,1},{1,2},{2,3},{3,0},{4,5},{5,6},{6,7},{7,4},{8,9},{9,10},{10,1... | collective-permute-start | bytes 3145736 | tf_op jit(solution)/shard_map/ppermute | solution.py:52
  482.1 20.6 %collective-permute-start.8 = (bf16[512,1024]{1,0:T(8,128)(2,1)}, bf16[512,1024]{1,0:T(8,128)(2,1)}, u32[]{:S(2)}, u32[]{:S(2)}) collective-permute-start(bf16[512,1024]{1,0:T(8,128)(2,1)} %collective-permute-done.7), channel_id=1, source_target_pairs={{0,1},{1,2},{2,3},{3,0},{4,5},{5,6},{6,7},{7,4},{8,9},{9,10},{10,1... | collective-permute-start | bytes 3145736 | tf_op jit(solution)/shard_map/ppermute | solution.py:52
Sparse Core Ops, SparseCore 0:
  77.9 160.6 all-gather.1
